TPU v7x, 16 devices: a whole 2x2x2 slice. The times are simulated.
16 devices in a mesh: depth: 2 (over z), col: 2 (over y), row: 4 (over x, core).
Axes of the slice: x: 2, y: 2, z: 2, core: 2. Of those that a mesh axis runs over, the one named last changes fastest.
Arguments:
- a_mat: bfloat16 [3072, 3072], P(('row', 'depth'), 'col')
- b_mat: bfloat16 [3072, 3072], P(('row', 'depth'), 'col')
Outputs:
- output: bfloat16 [3072, 3072], P(('row', 'depth'), 'col')
All inputs are finite; a program needn't handle non-finite values.
Results may differ from a plain program's by a relative error of at most 0.001.
Values are sent between devices in bfloat16 or wider.
A program may use at most 1 GiB of HBM per device.

v0:
```python
import jax
import jax.numpy as jnp
from jax import lax
from jax.sharding import PartitionSpec as P, NamedSharding


def solution(mesh):
    depth_n = mesh.shape["depth"]
    col_n = mesh.shape["col"]
    row_n = mesh.shape["row"]
    row_ratio = row_n // col_n
    layer_steps = row_n // depth_n
    all_axes = ("depth", "col", "row")

    def linear(layer, col_idx, row_idx):
        return (layer * col_n + col_idx) * row_n + row_idx

    def first_k(layer, row_idx):
        return (row_idx + layer * layer_steps) % row_n

    b_start = [
        (linear(layer, col_idx, (first_k(layer, row_idx) + col_idx * row_ratio) % row_n), linear(layer, col_idx, row_idx))
        for layer in range(depth_n) for col_idx in range(col_n) for row_idx in range(row_n)
    ]
    a_start = [
        (linear(layer, (col_idx + first_k(layer, row_idx) // row_ratio) % col_n, row_idx), linear(layer, col_idx, row_idx))
        for layer in range(depth_n) for col_idx in range(col_n) for row_idx in range(row_n)
    ]
    a_after = [
        (linear(layer, (col_idx + first_k(layer, row_idx) // row_ratio + 1) % col_n, row_idx), linear(layer, col_idx, row_idx))
        for layer in range(depth_n) for col_idx in range(col_n) for row_idx in range(row_n)
    ]
    b_shift = [((row_idx + 1) % row_n, row_idx) for row_idx in range(row_n)]
    a_shift = [((col_idx + 1) % col_n, col_idx) for col_idx in range(col_n)]

    def local_product(a_blk, b_blk):
        a_full = lax.all_gather(a_blk, "depth", axis=0, tiled=True)
        b_full = lax.all_gather(b_blk, "depth", axis=0, tiled=True)
        piece_w = a_full.shape[0]
        col_w = a_full.shape[1]
        b_cur = lax.ppermute(b_full, all_axes, b_start)
        a_lead = lax.ppermute(a_full, all_axes, a_start)
        if row_ratio == 1:
            queue = a_lead
        else:
            a_tail = lax.ppermute(a_full, all_axes, a_after)
            offset = (lax.axis_index("row") + lax.axis_index("depth") * layer_steps) % row_n % row_ratio
            joined = jnp.concatenate([a_lead, a_tail], axis=1)
            queue = lax.dynamic_slice_in_dim(joined, offset * piece_w, col_w, axis=1)
        pieces = [queue[:, slot * piece_w:(slot + 1) * piece_w] for slot in range(min(row_ratio, layer_steps))]
        part_sum = jnp.dot(pieces[0], b_cur, preferred_element_type=jnp.float32)
        for step in range(1, layer_steps):
            if step - 1 + row_ratio < layer_steps:
                pieces = pieces[1:] + [lax.ppermute(pieces[0], "col", a_shift)]
            else:
                pieces = pieces[1:]
            b_cur = lax.ppermute(b_cur, "row", b_shift)
            part_sum = part_sum + jnp.dot(pieces[0], b_cur, preferred_element_type=jnp.float32)
        c_part = lax.psum_scatter(part_sum, "depth", scatter_dimension=0, tiled=True)
        return c_part.astype(jnp.bfloat16)

    block_spec = P(("row", "depth"), "col")
    return jax.shard_map(local_product, mesh=mesh, in_specs=(block_spec, block_spec), out_specs=block_spec, check_vma=False)
```

profile of v0, /device:TPU:0, one launch (start us, length us, event | category | flops | bytes accessed | tf_op | source)
XLA Modules:
  0.0 216.2 jit_solution(15782435692951500492)
XLA Ops:
  6.5 0.0 all-gather.5.cloned.1.call-start
  6.5 0.7 all-gather.5.cloned.1.call-update
  7.3 0.0 all-gather.3.cloned.1.call-start
  7.3 0.7 all-gather.3.cloned.1.call-update
  8.0 0.0 reduce-scatter.2.cloned.1.call-start
  8.1 37.7 %all-gather.5.cloned.1.call-done = bf16[768,1536]{1,0:T(8,128)(2,1)} async-done(((bf16[384,1536]{1,0:T(8,128)(2,1)}), bf16[768,1536]{1,0:T(8,128)(2,1)}) %all-gather.5.cloned.1.call-update) | async-done | bytes 2359312 | tf_op jit(solution)/shard_map/all_gather | solution.py:38
  45.8 19.2 %collective-permute-start.2 = (bf16[768,1536]{1,0:T(8,128)(2,1)}, bf16[768,1536]{1,0:T(8,128)(2,1)}, u32[]{:S(2)}, u32[]{:S(2)}) collective-permute-start(bf16[768,1536]{1,0:T(8,128)(2,1)} %all-gather.5.cloned.1.call-done), channel_id=1, source_target_pairs={{0,0},{1,1},{2,2},{3,3},{6,4},{7,5},{4,6},{5,7},{10,8},{11,9},{8,1... | collective-permute-start | bytes 7077896 | tf_op jit(solution)/shard_map/ppermute | solution.py:41
  65.0 16.4 %all-gather.3.cloned.1.call-done = bf16[768,1536]{1,0:T(8,128)(2,1)} async-done(((bf16[384,1536]{1,0:T(8,128)(2,1)}), bf16[768,1536]{1,0:T(8,128)(2,1)}) %all-gather.3.cloned.1.call-update) | async-done | bytes 2359312 | tf_op jit(solution)/shard_map/all_gather | solution.py:37
  81.4 2.3 %collective-permute-start = (bf16[768,1536]{1,0:T(8,128)(2,1)}, bf16[768,1536]{1,0:T(8,128)(2,1)S(1)}, u32[]{:S(2)}, u32[]{:S(2)}) collective-permute-start(bf16[768,1536]{1,0:T(8,128)(2,1)} %all-gather.3.cloned.1.call-done), channel_id=1, source_target_pairs={{0,0},{1,1},{6,2},{7,3},{4,4},{5,5},{2,6},{3,7},{12,8},{13,9},{10,... | collective-permute-start | bytes 7077896 | tf_op jit(solution)/shard_map/ppermute | solution.py:42
  83.7 3.4 %collective-permute-start.1 = (bf16[768,1536]{1,0:T(8,128)(2,1)}, bf16[768,1536]{1,0:T(8,128)(2,1)}, u32[]{:S(2)}, u32[]{:S(2)}) collective-permute-start(bf16[768,1536]{1,0:T(8,128)(2,1)} %all-gather.3.cloned.1.call-done), channel_id=1, source_target_pairs={{4,0},{5,1},{2,2},{3,3},{0,4},{1,5},{6,6},{7,7},{8,8},{9,9},{14,10... | collective-permute-start | bytes 7077896 | tf_op jit(solution)/shard_map/ppermute | solution.py:46
  87.0 0.0 collective-permute-done.2
  87.1 17.3 %collective-permute-start.3 = (bf16[768,1536]{1,0:T(8,128)(2,1)}, bf16[768,1536]{1,0:T(8,128)(2,1)}, u32[]{:S(2)}, u32[]{:S(2)}) collective-permute-start(bf16[768,1536]{1,0:T(8,128)(2,1)} %collective-permute-done.2), channel_id=1, source_target_pairs={{1,0},{2,1},{3,2},{0,3},{5,4},{6,5},{7,6},{4,7},{9,8},{10,9},{11,1... | collective-permute-start | bytes 7077896 | tf_op jit(solution)/shard_map/ppermute | solution.py:57
  104.4 0.0 collective-permute-done
  104.4 33.9 %collective-permute-done.1 = bf16[768,1536]{1,0:T(8,128)(2,1)} collective-permute-done((bf16[768,1536]{1,0:T(8,128)(2,1)}, bf16[768,1536]{1,0:T(8,128)(2,1)}, u32[]{:S(2)}, u32[]{:S(2)}) %collective-permute-start.1) | collective-permute-done | bytes 2359328 | tf_op jit(solution)/shard_map/ppermute | solution.py:46
  138.3 0.8 fusion
  139.1 3.6 %fusion.2 = f32[768,1536]{1,0:T(8,128)S(1)} fusion(bf16[768,1536]{1,0:T(8,128)(2,1)} %collective-permute-done.2, bf16[768,1536]{1,0:T(8,128)(2,1)S(1)} %fusion), kind=kOutput, calls=%fused_computation.5 | convolution fusion | flops 1811939328 | bytes 8257536 | tf_op jit(solution)/shard_map/dot_general | solution.py:51
  142.8 0.0 collective-permute-done.3
  142.8 5.8 %convolution_add_fusion = f32[768,1536]{1,0:T(8,128)} fusion(f32[768,1536]{1,0:T(8,128)S(1)} %fusion.2, bf16[768,1536]{1,0:T(8,128)(2,1)} %collective-permute-done.3, bf16[768,1536]{1,0:T(8,128)(2,1)S(1)} %fusion), kind=kOutput, calls=%fused_computation.2 | convolution fusion | flops 1813118976 | bytes 12976128 | tf_op jit(solution)/shard_map/dot_general | solution.py:58
  148.6 0.0 reduce-scatter.2.cloned.1.call-update
  148.6 58.3 %reduce-scatter.2.cloned.1.call-done = f32[384,1536]{1,0:T(8,128)} async-done(((f32[768,1536]{1,0:T(8,128)}), f32[384,1536]{1,0:T(8,128)}) %reduce-scatter.2.cloned.1.call-update) | async-done | bytes 2359312 | tf_op jit(solution)/shard_map/reduce_scatter | solution.py:59
  206.9 2.8 %convert_element_type.3 = bf16[384,1536]{1,0:T(8,128)(2,1)} convert(f32[384,1536]{1,0:T(8,128)} %reduce-scatter.2.cloned.1.call-done) | non-fusion elementwise | flops 589824 | bytes 3538944 | tf_op jit(solution)/shard_map/convert_element_type | solution.py:60
Async XLA Ops:
  6.5 39.2 %all-gather.5.cloned.1.call-start = ((), (), s32[]{:S(2)}) async-start(), calls=%async_computation.2 | async-start | bytes 3538944 | tf_op jit(solution)/shard_map/all_gather | solution.py:38
  7.3 74.1 %all-gather.3.cloned.1.call-start = ((), (), s32[]{:S(2)}) async-start(), calls=%async_computation.1 | async-start | bytes 3538944 | tf_op jit(solution)/shard_map/all_gather | solution.py:37
  8.0 198.9 %reduce-scatter.2.cloned.1.call-start = ((), (), s32[]{:S(2)}) async-start(), calls=%async_computation.3 | async-start | bytes 7077888 | tf_op jit(solution)/shard_map/reduce_scatter | solution.py:59
  45.8 41.3 %collective-permute-start.2 = (bf16[768,1536]{1,0:T(8,128)(2,1)}, bf16[768,1536]{1,0:T(8,128)(2,1)}, u32[]{:S(2)}, u32[]{:S(2)}) collective-permute-start(bf16[768,1536]{1,0:T(8,128)(2,1)} %all-gather.5.cloned.1.call-done), channel_id=1, source_target_pairs={{0,0},{1,1},{2,2},{3,3},{6,4},{7,5},{4,6},{5,7},{10,8},{11,9},{8,1... | collective-permute-start | bytes 7077896 | tf_op jit(solution)/shard_map/ppermute | solution.py:41
  81.4 23.0 %collective-permute-start = (bf16[768,1536]{1,0:T(8,128)(2,1)}, bf16[768,1536]{1,0:T(8,128)(2,1)S(1)}, u32[]{:S(2)}, u32[]{:S(2)}) collective-permute-start(bf16[768,1536]{1,0:T(8,128)(2,1)} %all-gather.3.cloned.1.call-done), channel_id=1, source_target_pairs={{0,0},{1,1},{6,2},{7,3},{4,4},{5,5},{2,6},{3,7},{12,8},{13,9},{10,... | collective-permute-start | bytes 7077896 | tf_op jit(solution)/shard_map/ppermute | solution.py:42
  83.7 54.6 %collective-permute-start.1 = (bf16[768,1536]{1,0:T(8,128)(2,1)}, bf16[768,1536]{1,0:T(8,128)(2,1)}, u32[]{:S(2)}, u32[]{:S(2)}) collective-permute-start(bf16[768,1536]{1,0:T(8,128)(2,1)} %all-gather.3.cloned.1.call-done), channel_id=1, source_target_pairs={{4,0},{5,1},{2,2},{3,3},{0,4},{1,5},{6,6},{7,7},{8,8},{9,9},{14,10... | collective-permute-start | bytes 7077896 | tf_op jit(solution)/shard_map/ppermute | solution.py:46
  87.1 55.7 %collective-permute-start.3 = (bf16[768,1536]{1,0:T(8,128)(2,1)}, bf16[768,1536]{1,0:T(8,128)(2,1)}, u32[]{:S(2)}, u32[]{:S(2)}) collective-permute-start(bf16[768,1536]{1,0:T(8,128)(2,1)} %collective-permute-done.2), channel_id=1, source_target_pairs={{1,0},{2,1},{3,2},{0,3},{5,4},{6,5},{7,6},{4,7},{9,8},{10,9},{11,1... | collective-permute-start | bytes 7077896 | tf_op jit(solution)/shard_map/ppermute | solution.py:57
Sparse Core Ops, SparseCore 0:
  8.8 36.8 all-gather.4
  47.3 34.0 all-gather.2
  148.8 58.0 reduce-scatter.1
where the time goes:
time: 219 us; the launch traced here: 216 us
  waiting for transfers between devices  148 us (68%)
  starting transfers between devices  42.3 us (19%)
  between operations  13.1 us (6%)
  matrix products  9.45 us (4%)
  other arithmetic  3.65 us (2%)
    reduce_scatter x1, waiting for transfers between devices, local_product(): lax.psum_scatter(part_sum, 'depth', scatter_dimension=0, tiled=True)  58.3 us
    all_gather x1, waiting for transfers between devices, local_product(): b_full = lax.all_gather(b_blk, 'depth', axis=0, tiled=True)  37.7 us
    ppermute x1, waiting for transfers between devices, local_product(): a_tail = lax.ppermute(a_full, all_axes, a_after)  33.9 us
    ppermute x1, starting transfers between devices, local_product(): b_cur = lax.ppermute(b_full, all_axes, b_start)  19.2 us
    ppermute x1, starting transfers between devices, local_product(): b_cur = lax.ppermute(b_cur, 'row', b_shift)  17.3 us
    all_gather x1, waiting for transfers between devices, local_product(): a_full = lax.all_gather(a_blk, 'depth', axis=0, tiled=True)  16.4 us
    dot_general x1, matrix products, local_product(): jnp.dot(pieces[0], b_cur, preferred_element_type=jnp.float32)  5.8 us
  transfers between devices with their start and end apart: 7, of which 4 were waited for; matrix products, arithmetic and copies ran while one was open for 2% of the time, Pallas kernels for 0%

commit v1 on v0

v1 whole, which is shorter than its diff:
```python
import functools

import jax
import jax.numpy as jnp
from jax import lax
from jax.experimental import pallas as pl
from jax.experimental.pallas import tpu as pltpu
from jax.sharding import PartitionSpec as P

MESH = pl.DeviceIdType.MESH
BLOCKS = 6


def kernel(blocks, a_hbm, b_hbm, c_ref, a_buf, b_buf, total,
           a_in, b_in, xs, xr, zs, zr, ys, yr, fxs, fxr, fzs, fzr,
           pos, por, pxs, pxr, pzs, pzr, pas, par, pbs, pbr):
    z = lax.axis_index("depth")
    y = lax.axis_index("col")
    row = lax.axis_index("row")
    x = row // 2
    c = row % 2
    ox, oy, oz = 1 - x, 1 - y, 1 - z
    rows, width = b_buf.shape[4], b_buf.shape[5]
    half = rows // 2
    partner = (z, y, 2 * x + 1 - c)
    x_dev = (z, y, 2 * ox + c)
    y_dev = (z, oy, row)
    z_dev = (oz, y, row)
    lo, hi = pl.ds(0, half), pl.ds(half, half)

    def remote(src, dst, send, recv, dev):
        return pltpu.make_async_remote_copy(
            src_ref=src, dst_ref=dst, send_sem=send, recv_sem=recv,
            device_id=dev, device_id_type=MESH)

    def same(ref, send, recv, dev):
        return remote(ref, ref, send, recv, dev)

    b_loads = [pltpu.make_async_copy(
        b_hbm.at[:, pl.ds(b * width, width)], b_buf.at[x, z, b, c], b_in.at[b]) for b in range(blocks)]
    a_loads = [pltpu.make_async_copy(
        a_hbm.at[:, pl.ds(q * rows, rows)], a_buf.at[y, q % 2, q // 2], a_in.at[q]) for q in range(4)]
    for load in b_loads + a_loads:
        load.start()

    barrier = pltpu.get_barrier_semaphore()
    for dev in (partner, x_dev, y_dev, z_dev):
        pl.semaphore_signal(barrier, inc=1, device_id=dev, device_id_type=MESH)
    pl.semaphore_wait(barrier, 4)

    sends = []

    def go(copy):
        copy.start()
        sends.append(copy)

    for b in range(blocks):
        b_loads[b].wait()
        go(same(b_buf.at[x, z, b, c], xs.at[b], xr.at[b], x_dev))
        go(same(b_buf.at[x, z, b, c], zs.at[b], zr.at[b], z_dev))
        if b == 0:
            for load in a_loads:
                load.wait()
            go(same(a_buf.at[y], ys, yr, y_dev))
        go(same(b_buf.at[x, z, b, c], pos.at[b], por.at[b], partner))

    for b in range(blocks):
        same(b_buf.at[x, oz, b, c], zs.at[b], zr.at[b], z_dev).wait_recv()
        go(same(b_buf.at[x, oz, b, c, lo], fxs.at[b], fxr.at[b], x_dev))
        go(same(b_buf.at[x, oz, b, c], pzs.at[b], pzr.at[b], partner))
        same(b_buf.at[ox, z, b, c], xs.at[b], xr.at[b], x_dev).wait_recv()
        go(same(b_buf.at[ox, z, b, c, hi], fzs.at[b], fzr.at[b], z_dev))
        go(same(b_buf.at[ox, z, b, c], pxs.at[b], pxr.at[b], partner))

    same(a_buf.at[oy], ys, yr, y_dev).wait_recv()
    for b in range(blocks):
        same(b_buf.at[x, z, b, 1 - c], pos.at[b], por.at[b], partner).wait_recv()
        same(b_buf.at[x, oz, b, 1 - c], pzs.at[b], pzr.at[b], partner).wait_recv()
        same(b_buf.at[ox, z, b, 1 - c], pxs.at[b], pxr.at[b], partner).wait_recv()

    def product(xk, zk, b):
        lhs = jnp.concatenate([a_buf[xk, zk, 0], a_buf[xk, zk, 1]], axis=1)
        rhs = b_buf[xk, zk, b].reshape(2 * rows, width)
        return jnp.dot(lhs, rhs, preferred_element_type=jnp.float32)

    @pl.loop(0, blocks)
    def _(b):
        total[b] = product(x, z, b) + product(x, oz, b) + product(ox, z, b)

    for b in range(blocks):
        same(b_buf.at[ox, oz, b, c, lo], fxs.at[b], fxr.at[b], x_dev).wait_recv()
        go(same(b_buf.at[ox, oz, b, c, lo], pas.at[b], par.at[b], partner))
        same(b_buf.at[ox, oz, b, c, hi], fzs.at[b], fzr.at[b], z_dev).wait_recv()
        go(same(b_buf.at[ox, oz, b, c, hi], pbs.at[b], pbr.at[b], partner))
        same(b_buf.at[ox, oz, b, 1 - c, lo], pas.at[b], par.at[b], partner).wait_recv()
        same(b_buf.at[ox, oz, b, 1 - c, hi], pbs.at[b], pbr.at[b], partner).wait_recv()
        c_ref[:, pl.ds(b * width, width)] = (total[b] + product(ox, oz, b)).astype(c_ref.dtype)

    for copy in sends:
        copy.wait_send()


def solution(mesh):
    def local_product(a_blk, b_blk):
        rows, cols = a_blk.shape
        width = cols // BLOCKS
        dma = pltpu.SemaphoreType.DMA
        per_block = [dma((BLOCKS,))] * 2
        return pl.pallas_call(
            functools.partial(kernel, BLOCKS),
            out_shape=jax.ShapeDtypeStruct((rows, cols), jnp.bfloat16),
            in_specs=[pl.BlockSpec(memory_space=pl.ANY)] * 2,
            out_specs=pl.BlockSpec(memory_space=pltpu.VMEM),
            scratch_shapes=[
                pltpu.VMEM((2, 2, 2, rows, rows), jnp.bfloat16),
                pltpu.VMEM((2, 2, BLOCKS, 2, rows, width), jnp.bfloat16),
                pltpu.VMEM((BLOCKS, rows, width), jnp.float32),
                dma((4,)), dma((BLOCKS,)),
                *per_block, *per_block, dma, dma, *per_block, *per_block,
                *per_block, *per_block, *per_block, *per_block, *per_block,
            ],
            compiler_params=pltpu.CompilerParams(collective_id=0, has_side_effects=True),
        )(a_blk, b_blk)

    block_spec = P(("row", "depth"), "col")
    return jax.shard_map(local_product, mesh=mesh, in_specs=(block_spec, block_spec), out_specs=block_spec, check_vma=False)
```

time: 219 us -> 50.9 us (0.23); the launches traced: 216 us -> 50.6 us
  waiting for transfers between devices: 148 us -> 0 us
  Pallas kernels: 0 us -> 48.3 us
  starting transfers between devices: 42.3 us -> 0 us
  between operations: 13.1 us -> 0.01 us
  matrix products: 9.45 us -> 0 us
  other arithmetic: 3.65 us -> 0 us
  local copies, waits for them, and re-layouts: 0 us -> 2.36 us
    reduce_scatter x1 -> x0, waiting for transfers between devices: 58.3 us -> none  [local_product(): lax.psum_scatter(part_sum, 'depth', scatter_dimension=0, tiled=True)]
    all_gather x2 -> x0, waiting for transfers between devices: 54.1 us -> none  [the longest x1 37.7 us: local_product(): b_full = lax.all_gather(b_blk, 'depth', axis=0, tiled=True)]
    pallas_call x0 -> x1, Pallas kernels: none -> 48.3 us  [local_product(): pl.pallas_call(functools.partial(kernel, BLOCKS), out_shape=jax.ShapeDtyp...]
    ppermute x4 -> x0, starting transfers between devices: 42.2 us -> none  [the longest x1 19.2 us: local_product(): b_cur = lax.ppermute(b_full, all_axes, b_start)]
    ppermute x4 -> x0, waiting for transfers between devices: 33.9 us -> none  [the longest x1 33.9 us: local_product(): a_tail = lax.ppermute(a_full, all_axes, a_after)]
    dot_general x2 -> x0, matrix products: 9.45 us -> none  [the longest x1 5.8 us: local_product(): jnp.dot(pieces[0], b_cur, preferred_element_type=jnp.float32)]
    convert_element_type x1 -> x0, other arithmetic: 2.8 us -> none  [local_product(): return c_part.astype(jnp.bfloat16)]
    unnamed x0 -> x1, local copies, waits for them, and re-layouts: none -> 2.36 us
  transfers between devices with their start and end apart: 7 -> 0, of which waited for: 4 -> 0; matrix products, arithmetic and copies ran while one was open for 2% -> 0% of each run, Pallas kernels for 0% -> 0%
where the time goes in v1:
time: 50.9 us; the launch traced here: 50.6 us
  Pallas kernels  48.3 us (95%)
  local copies, waits for them, and re-layouts  2.36 us (5%)
    pallas_call x1, Pallas kernels, local_product(): pl.pallas_call(functools.partial(kernel, BLOCKS), out_shape=jax.ShapeDtyp...  48.3 us
    unnamed x1, local copies, waits for them, and re-layouts  2.36 us

profile of v1, /device:TPU:0, one launch (start us, length us, event | category | flops | bytes accessed | tf_op | source)
XLA Modules:
  0.0 50.6 jit_solution(14531368146488272589)
XLA Ops:
  0.0 48.3 %shard_map.28 = bf16[384,1536]{1,0:T(8,128)(2,1)} custom-call(bf16[384,1536]{1,0:T(8,128)(2,1)} %a_hbm.1, bf16[384,1536]{1,0:T(8,128)(2,1)} %b_hbm.1), custom_call_target="tpu_custom_call" | custom-call | tf_op jit(solution)/shard_map/pallas_call | solution.py:109
  48.3 2.4 %copy.4 = bf16[384,1536]{1,0:T(8,128)(2,1)} copy(bf16[384,1536]{1,0:T(8,128)(2,1)} %shard_map.28) | data formatting | bytes 2359296

commit v2 on v1

--- a/solution.py
+++ b/solution.py
@@ -8,7 +8,7 @@
 from jax.sharding import PartitionSpec as P
 
 MESH = pl.DeviceIdType.MESH
-BLOCKS = 6
+BLOCKS = 3
 
 
 def kernel(blocks, a_hbm, b_hbm, c_ref, a_buf, b_buf, total,

time: 50.9 us -> 48.7 us (0.957)
  Pallas kernels: 48.3 us -> 46.1 us
    pallas_call x1, Pallas kernels: 48.3 us -> 46.1 us  [local_product(): pl.pallas_call(functools.partial(kernel, BLOCKS), out_shape=jax.ShapeDtyp...]
where the time goes in v2:
time: 48.7 us; the launch traced here: 48.4 us
  Pallas kernels  46.1 us (95%)
  local copies, waits for them, and re-layouts  2.36 us (5%)
    pallas_call x1, Pallas kernels, local_product(): pl.pallas_call(functools.partial(kernel, BLOCKS), out_shape=jax.ShapeDtyp...  46.1 us
    unnamed x1, local copies, waits for them, and re-layouts  2.36 us

profile of v2, /device:TPU:0, one launch (start us, length us, event | category | flops | bytes accessed | tf_op | source)
XLA Modules:
  0.0 48.4 jit_solution(5503791151789752498)
XLA Ops:
  0.0 46.1 %shard_map.28 = bf16[384,1536]{1,0:T(8,128)(2,1)} custom-call(bf16[384,1536]{1,0:T(8,128)(2,1)} %a_hbm.1, bf16[384,1536]{1,0:T(8,128)(2,1)} %b_hbm.1), custom_call_target="tpu_custom_call" | custom-call | tf_op jit(solution)/shard_map/pallas_call | solution.py:109
  46.1 2.4 %copy.4 = bf16[384,1536]{1,0:T(8,128)(2,1)} copy(bf16[384,1536]{1,0:T(8,128)(2,1)} %shard_map.28) | data formatting | bytes 2359296

commit v3 on v2

--- a/solution.py
+++ b/solution.py
@@ -108,7 +108,7 @@
         per_block = [dma((BLOCKS,))] * 2
         return pl.pallas_call(
             functools.partial(kernel, BLOCKS),
-            out_shape=jax.ShapeDtypeStruct((rows, cols), jnp.bfloat16),
+            out_shape=pltpu.VMEM((rows, cols), jnp.bfloat16),
             in_specs=[pl.BlockSpec(memory_space=pl.ANY)] * 2,
             out_specs=pl.BlockSpec(memory_space=pltpu.VMEM),
             scratch_shapes=[

time: 48.7 us -> 46.3 us (0.951)
  local copies, waits for them, and re-layouts: 2.36 us -> 1.02 us
  Pallas kernels: 46.1 us -> 45 us
    unnamed x1, local copies, waits for them, and re-layouts: 2.36 us -> 1.02 us
    pallas_call x1, Pallas kernels: 46.1 us -> 45 us  [local_product(): pl.pallas_call(functools.partial(kernel, BLOCKS), out_shape=pltpu.VMEM((r...]
where the time goes in v3:
time: 46.3 us; the launch traced here: 46.1 us
  Pallas kernels  45 us (97%)
  local copies, waits for them, and re-layouts  1.02 us (2%)
    pallas_call x1, Pallas kernels, local_product(): pl.pallas_call(functools.partial(kernel, BLOCKS), out_shape=pltpu.VMEM((r...  45 us
    unnamed x1, local copies, waits for them, and re-layouts  1.02 us

profile of v3, /device:TPU:0, one launch (start us, length us, event | category | flops | bytes accessed | tf_op | source)
XLA Modules:
  0.0 46.1 jit_solution(371445751119202762)
XLA Ops:
  0.0 45.0 %shard_map.28 = bf16[384,1536]{1,0:T(8,128)(2,1)S(1)} custom-call(bf16[384,1536]{1,0:T(8,128)(2,1)} %a_hbm.1, bf16[384,1536]{1,0:T(8,128)(2,1)} %b_hbm.1), custom_call_target="tpu_custom_call" | custom-call | tf_op jit(solution)/shard_map/pallas_call | solution.py:109
  45.1 1.0 %copy.4 = bf16[384,1536]{1,0:T(8,128)(2,1)} copy(bf16[384,1536]{1,0:T(8,128)(2,1)S(1)} %shard_map.28) | data formatting | bytes 2359296
